TPU v7x, 32 devices: a whole 2x2x4 slice. The times are simulated.
32 devices in a mesh: row: 8 (over z, x), col: 4 (over y, core).
Axes of the slice: x: 2, y: 2, z: 4, core: 2. Of those that a mesh axis runs over, the one named last changes fastest.
Arguments:
- pair: bfloat16 [64, 64, 128], P('row', 'col'), may hold values from -6 to 6
- norm_in: float32 [128], replicated, may hold values from 0.1 to 1.9
- shift_in: float32 [128], replicated, may hold values from -3 to 3
- in_weight: bfloat16 [128, 640], replicated, may hold values from -0.5 to 0.5
- norm_out: float32 [128], replicated, may hold values from 0.1 to 1.9
- shift_out: float32 [128], replicated, may hold values from -3 to 3
- out_weight: bfloat16 [128, 128], replicated, may hold values from -0.5 to 0.5
Outputs:
- update: bfloat16 [64, 64, 128], P('row', 'col')
All inputs are finite; a program needn't handle non-finite values.
Results may differ from a plain program's by a relative error of at most 0.0054.
Values may be sent and summed in bfloat16 or wider, within the bound.
A program may use at most 64 MiB of HBM per device.

v0:
```python
import jax
import jax.numpy as jnp
from jax import lax
from jax.sharding import PartitionSpec as P

EPSILON = 1e-05


def layer_norm(values, gain, shift):
    values = values.astype(jnp.float32)
    center = jnp.mean(values, axis=-1, keepdims=True)
    spread = jnp.mean(jnp.square(values - center), axis=-1, keepdims=True)
    return (values - center) * lax.rsqrt(spread + EPSILON) * gain + shift


def local(pair, norm_in, shift_in, in_weight, norm_out, shift_out, out_weight):
    row_count, col_count, channels = pair.shape
    hidden = out_weight.shape[0]
    normed = layer_norm(pair, norm_in, shift_in).astype(jnp.bfloat16)
    projected = jnp.dot(normed.reshape(-1, channels), in_weight, preferred_element_type=jnp.float32)
    left = (jax.nn.sigmoid(projected[:, :hidden]) * projected[:, hidden : 2 * hidden]).astype(
        jnp.bfloat16
    )
    right = (
        jax.nn.sigmoid(projected[:, 2 * hidden : 3 * hidden])
        * projected[:, 3 * hidden : 4 * hidden]
    ).astype(jnp.bfloat16)
    gate = jax.nn.sigmoid(projected[:, 4 * hidden :]).reshape(row_count, col_count, channels)
    left = left.reshape(row_count, col_count, hidden)
    right = right.reshape(row_count, col_count, hidden)
    row_devices = lax.axis_size("row")
    col_devices = lax.axis_size("col")
    unit = row_count // col_devices
    groups = row_devices // col_devices
    sectioned = left.reshape(row_count, groups, col_devices, unit, hidden).transpose(0, 2, 1, 3, 4)
    sorted_parts = lax.all_to_all(sectioned, "col", split_axis=1, concat_axis=1, tiled=True)
    sorted_parts = sorted_parts.reshape(row_count, row_devices, unit * hidden)
    own_parts = lax.all_to_all(sorted_parts, "row", split_axis=1, concat_axis=0, tiled=True)
    own_parts = own_parts.reshape(row_count * row_devices, unit, hidden)
    right_full = lax.all_gather(right, "row", axis=0, tiled=True)
    mixed = jnp.einsum(
        "kih,kjh->ijh",
        lax.all_gather(own_parts, "col", axis=1, tiled=True),
        right_full,
        preferred_element_type=jnp.float32,
    )
    mixed_normed = layer_norm(mixed, norm_out, shift_out).astype(jnp.bfloat16)
    outward = jnp.dot(
        mixed_normed.reshape(-1, hidden), out_weight, preferred_element_type=jnp.float32
    )
    return (gate * outward.reshape(row_count, col_count, channels)).astype(jnp.bfloat16)


def solution(mesh):
    in_specs = (P("row", "col", None), P(), P(), P(), P(), P(), P())
    out_specs = P("row", "col", None)
    return jax.shard_map(local, mesh=mesh, in_specs=in_specs, out_specs=out_specs, check_vma=False)
```

profile of v0, /device:TPU:0, one launch (start us, length us, event | category | flops | bytes accessed | tf_op | source)
XLA Modules:
  0.0 71.7 jit_solution(3137486336146539258)
XLA Ops:
  0.0 0.0 copy-start
  0.0 0.9 %convert_reduce_fusion = f32[8,16]{1,0:T(8,128)S(1)} fusion(bf16[8,16,128]{2,1,0:T(8,128)(2,1)} %param.7), kind=kLoop, calls=%fused_computation.3 | loop fusion | flops 32640 | bytes 33280 | tf_op jit(solution)/shard_map/reduce_sum | solution.py:11
  0.9 0.9 %fusion.3 = f32[8,16]{1,0:T(8,128)S(1)} fusion(bf16[8,16,128]{2,1,0:T(8,128)(2,1)} %param.7, f32[8,16]{1,0:T(8,128)S(1)} %broadcast_multiply_fusion.1), kind=kLoop, calls=%fused_computation.6 | loop fusion | flops 65408 | bytes 33792 | tf_op jit(solution)/shard_map/reduce_sum | solution.py:12
  1.8 0.9 %fusion.6 = bf16[8,16,128]{2,1,0:T(8,128)(2,1)S(1)} fusion(bf16[8,16,128]{2,1,0:T(8,128)(2,1)} %param.7, f32[128]{0:T(128)} %param.9, f32[128]{0:T(128)} %param.8, f32[8,16]{1,0:T(8,128)S(1)} %add_rsqrt_fusion.1, f32[8,16]{1,0:T(8,128)S(1)} %broadcast_multiply_fusion.1), kind=kLoop, calls=%fused_computation.9 | loop fusion | flops 98304 | bytes 67584 | tf_op jit(solution)/shard_map/convert_element_type | solution.py:19
  2.7 0.0 copy-done
  2.7 0.2 fusion.23
  2.9 0.1 fusion.7
  3.0 0.6 copy.32
  3.6 4.3 %all-to-all-start = ((bf16[8,4,2,2,128]{4,3,2,0,1:T(2,128)(2,1)}), bf16[8,4,2,2,128]{4,3,2,0,1:T(2,128)(2,1)S(1)}, u32[]{:S(2)}, u32[]{:S(2)}) async-start(bf16[8,4,2,2,128]{4,3,2,0,1:T(2,128)(2,1)} %bitcast.30), calls=%async_computation | async-start | bytes 65536 | tf_op jit(solution)/shard_map/all_to_all | solution.py:36
  7.9 0.2 copy.22
  8.1 3.8 %all-to-all-done = bf16[8,4,2,2,128]{4,3,2,0,1:T(2,128)(2,1)S(1)} async-done(((bf16[8,4,2,2,128]{4,3,2,0,1:T(2,128)(2,1)}), bf16[8,4,2,2,128]{4,3,2,0,1:T(2,128)(2,1)S(1)}, u32[]{:S(2)}, u32[]{:S(2)}) %all-to-all-start) | async-done | bytes 32800 | tf_op jit(solution)/shard_map/all_to_all | solution.py:36
  11.9 0.6 reshape.54
  12.5 6.3 %all-to-all-start.1 = ((bf16[8,8,256]{2,0,1:T(8,128)(2,1)}), bf16[8,8,256]{2,0,1:T(8,128)(2,1)S(1)}, u32[]{:S(2)}, u32[]{:S(2)}) async-start(bf16[8,8,256]{2,0,1:T(8,128)(2,1)} %reshape.54), calls=%async_computation.1 | async-start | bytes 65536 | tf_op jit(solution)/shard_map/all_to_all | solution.py:38
  18.8 45.2 %all_gather.6 = bf16[64,16,128]{1,0,2:T(8,128)(2,1)S(1)} all-gather(bf16[8,16,128]{1,0,2:T(8,128)(2,1)S(1)} %copy.22), channel_id=1, replica_groups=mesh['row'=8,'col'=4] {'row'}, dimensions={0}, use_global_device_ids=true | all-gather | bytes 294912 | tf_op jit(solution)/shard_map/all_gather | solution.py:40
  64.0 0.0 all-to-all-done.1
  64.0 0.0 copy-start.1
  64.1 0.0 copy-start.2
  64.1 0.0 copy-start.3
  64.1 5.4 %all_gather.7 = bf16[64,8,128]{2,0,1:T(8,128)(2,1)S(1)} all-gather(bf16[64,2,128]{2,0,1:T(8,128)(2,1)S(1)} %copy.26), channel_id=1, replica_groups=mesh['row'=8,'col'=4] {'col'}, dimensions={1}, use_global_device_ids=true | all-gather | bytes 163840 | tf_op jit(solution)/shard_map/all_gather | solution.py:43
  69.5 0.2 copy.27
  69.7 0.7 fusion.24
  70.3 0.2 copy.28
  70.5 0.1 bitcast_reduce_fusion
  70.7 0.2 multiply_reduce_fusion
  70.8 0.0 copy-done.1
  70.9 0.0 copy-done.2
  70.9 0.0 copy-done.3
  70.9 0.8 %fusion = bf16[8,16,128]{2,1,0:T(8,128)(2,1)} fusion(f32[8,16,128]{2,1,0:T(8,128)S(1)} %bitcast.31, f32[128,16,8]{0,1,2:T(8,128)S(1)} %copy.28, bf16[128,128]{1,0:T(8,128)(2,1)S(1)} %copy-done.1, f32[128]{0:T(128)S(1)} %copy-done.2, f32[128]{0:T(128)S(1)} %copy-done.3, f32[8,16]{1,0:T(8,128)S(1)} %add_rsqrt_fusion, f32[8,16]{1,0:T(8,128)S(1)} %broadcast_multiply_fusion), kind=kOutput, calls=%fused_computation.1 | convolution fusion | flops 4308992 | bytes 198656 | tf_op jit(solution)/shard_map/dot_general | solution.py:48
  (7 shorter events, 0.1 us)
Async XLA Ops:
  0.0 2.7 %copy-start = (bf16[128,640]{1,0:T(8,128)(2,1)S(1)}, bf16[128,640]{1,0:T(8,128)(2,1)}, u32[]{:S(2)}) copy-start(bf16[128,640]{1,0:T(8,128)(2,1)} %param.10) | copy-start | bytes 491524
  3.6 8.2 %all-to-all-start = ((bf16[8,4,2,2,128]{4,3,2,0,1:T(2,128)(2,1)}), bf16[8,4,2,2,128]{4,3,2,0,1:T(2,128)(2,1)S(1)}, u32[]{:S(2)}, u32[]{:S(2)}) async-start(bf16[8,4,2,2,128]{4,3,2,0,1:T(2,128)(2,1)} %bitcast.30), calls=%async_computation | async-start | bytes 65536 | tf_op jit(solution)/shard_map/all_to_all | solution.py:36
  12.5 51.5 %all-to-all-start.1 = ((bf16[8,8,256]{2,0,1:T(8,128)(2,1)}), bf16[8,8,256]{2,0,1:T(8,128)(2,1)S(1)}, u32[]{:S(2)}, u32[]{:S(2)}) async-start(bf16[8,8,256]{2,0,1:T(8,128)(2,1)} %reshape.54), calls=%async_computation.1 | async-start | bytes 65536 | tf_op jit(solution)/shard_map/all_to_all | solution.py:38
  64.0 6.8 %copy-start.1 = (bf16[128,128]{1,0:T(8,128)(2,1)S(1)}, bf16[128,128]{1,0:T(8,128)(2,1)}, u32[]{:S(2)}) copy-start(bf16[128,128]{1,0:T(8,128)(2,1)} %param.13) | copy-start | bytes 98308
  64.1 6.8 %copy-start.2 = (f32[128]{0:T(128)S(1)}, f32[128]{0:T(128)}, u32[]{:S(2)}) copy-start(f32[128]{0:T(128)} %param.12) | copy-start | bytes 1540
  64.1 6.8 %copy-start.3 = (f32[128]{0:T(128)S(1)}, f32[128]{0:T(128)}, u32[]{:S(2)}) copy-start(f32[128]{0:T(128)} %param.11) | copy-start | bytes 1540
where the time goes:
time: 72.2 us; the launch traced here: 71.7 us
  blocking collectives  50.7 us (70%)
  starting transfers between devices  10.5 us (15%)
  waiting for transfers between devices  3.76 us (5%)
  other arithmetic  3.04 us (4%)
  local copies, waits for them, and re-layouts  1.92 us (3%)
  matrix products  1.67 us (2%)
    all_gather x1, blocking collectives, local(): right_full = lax.all_gather(right, 'row', axis=0, tiled=True)  45.2 us
    all_to_all x1, starting transfers between devices, local(): lax.all_to_all(sorted_parts, 'row', split_axis=1, concat_axis=0, tiled=True)  6.25 us
    all_gather x1, blocking collectives, local(): lax.all_gather(own_parts, 'col', axis=1, tiled=True)  5.42 us
    all_to_all x1, starting transfers between devices, local(): lax.all_to_all(sectioned, 'col', split_axis=1, concat_axis=1, tiled=True)  4.26 us
    all_to_all x1, waiting for transfers between devices, local(): lax.all_to_all(sectioned, 'col', split_axis=1, concat_axis=1, tiled=True)  3.76 us
  transfers between devices with their start and end apart: 2, of which 1 were waited for; matrix products, arithmetic and copies ran while one was open for 0% of the time, Pallas kernels for 0%

commit v1 on v0

v1 whole, which is shorter than its diff:
```python
import functools

import jax
import jax.numpy as jnp
from jax import lax
from jax.experimental import pallas as pl
from jax.experimental.pallas import tpu as pltpu
from jax.sharding import PartitionSpec as P

EPSILON = 1e-05
MESH = pl.DeviceIdType.MESH


def layer_norm(values, gain, shift):
    center = jnp.mean(values, axis=-1, keepdims=True)
    values = values - center
    spread = jnp.mean(jnp.square(values), axis=-1, keepdims=True)
    return values * lax.rsqrt(spread + EPSILON) * gain + shift


def fit(size, most):
    while size % most:
        most -= 1
    return most


def loop(count, body):
    if count == 1:
        body(0)
    else:
        pl.loop(0, count)(body)


def kernel(
    n_row, n_col, pair_ref, gain_in, shift_in, w_in, gain_out, shift_out, w_out, out_ref,
    left_own, left_all, right_all, gate_ref, mixed, left_send, left_recv, right_send, right_recv,
):
    rows, cols, channels = pair_ref.shape
    hidden = w_out.shape[0]
    groups = n_row // n_col
    r, c = lax.axis_index("row"), lax.axis_index("col")
    home = r // groups

    barrier = pltpu.get_barrier_semaphore()

    def greet(row, col):
        pl.semaphore_signal(barrier, inc=1, device_id=(row, col), device_id_type=MESH)

    @pl.loop(1, n_row)
    def _(d):
        greet(lax.rem(r + d, n_row), c)

    @pl.loop(0, n_row)
    def _(d):
        row = lax.rem(r + d, n_row)

        @pl.when(jnp.logical_or(row != r, home != c))
        def _():
            greet(row, home)

    step = fit(rows, max(1, 128 // cols))

    def project(t):
        at = pl.ds(t * step, step)
        block = pair_ref[at].reshape(step * cols, channels).astype(jnp.float32)
        normed = layer_norm(block, gain_in[...], shift_in[...]).astype(jnp.bfloat16)

        def part(index):
            return jnp.dot(
                normed, w_in[:, index * hidden : (index + 1) * hidden],
                preferred_element_type=jnp.float32,
            )

        left = (jax.nn.sigmoid(part(0)) * part(1)).astype(jnp.bfloat16).reshape(step, cols, hidden)
        for g in range(groups):
            left_own[g, at] = left[:, g * rows : (g + 1) * rows]
        right = (jax.nn.sigmoid(part(2)) * part(3)).astype(jnp.bfloat16)
        right_all[r, at] = right.reshape(step, cols, hidden)
        gate_ref[at] = jax.nn.sigmoid(part(4)).reshape(step, cols, channels)

    loop(rows // step, project)

    own = jnp.where(home == c, 1, 0)
    pl.semaphore_wait(barrier, n_row - 1 + groups * n_col - own)

    def right_copy(d):
        return pltpu.make_async_remote_copy(
            src_ref=right_all.at[r], dst_ref=right_all.at[r],
            send_sem=right_send.at[d], recv_sem=right_recv.at[r],
            device_id=(lax.rem(r + d, n_row), c), device_id_type=MESH,
        )

    def left_copy(g, d):
        return pltpu.make_async_remote_copy(
            src_ref=left_own.at[g], dst_ref=left_all.at[r],
            send_sem=left_send.at[g * n_col + d], recv_sem=left_recv.at[r],
            device_id=(c * groups + g, lax.rem(c + d, n_col)), device_id_type=MESH,
        )

    def each_left(act):
        for g in range(groups):
            @pl.loop(0, n_col)
            def _(d):
                @pl.when(jnp.logical_or(d != 0, r != c * groups + g))
                def _():
                    act(left_copy(g, d))

    each_left(lambda copy: copy.start())

    @pl.loop(1, n_row)
    def _(d):
        right_copy(d).start()

    for g in range(groups):
        @pl.when(r == c * groups + g)
        def _():
            left_all[r] = left_own[g]

    tile_k, tile_i, tile_j = fit(rows, 8), fit(rows, 8), fit(cols, 16)
    mixed[...] = jnp.zeros_like(mixed)

    def accumulate(s):
        def over_i(ti):
            def over_j(tj):
                here = (pl.ds(ti * tile_i, tile_i), pl.ds(tj * tile_j, tile_j))

                def over_k(tk):
                    ks = pl.ds(tk * tile_k, tile_k)
                    lefts = left_all[s, ks, here[0]].astype(jnp.float32)
                    rights = right_all[s, ks, here[1]].astype(jnp.float32)
                    total = mixed[here]
                    for k in range(tile_k):
                        total += lefts[k][:, None, :] * rights[k][None]
                    mixed[here] = total

                loop(rows // tile_k, over_k)

            loop(cols // tile_j, over_j)

        loop(rows // tile_i, over_i)

    @pl.loop(0, n_row)
    def _(d):
        s = lax.rem(r + n_row - d, n_row)

        @pl.when(d != 0)
        def _():
            pltpu.make_async_copy(right_all.at[s], right_all.at[s], right_recv.at[s]).wait()

        @pl.when(jnp.logical_or(d != 0, home != c))
        def _():
            pltpu.make_async_copy(left_all.at[s], left_all.at[s], left_recv.at[s]).wait()

        accumulate(s)

    def finish(t):
        at = pl.ds(t * step, step)
        normed = layer_norm(
            mixed[at].reshape(step * cols, hidden), gain_out[...], shift_out[...]
        ).astype(jnp.bfloat16)
        outward = jnp.dot(normed, w_out[...], preferred_element_type=jnp.float32)
        out_ref[at] = (gate_ref[at] * outward.reshape(step, cols, channels)).astype(jnp.bfloat16)

    loop(rows // step, finish)

    each_left(lambda copy: copy.wait_send())

    @pl.loop(1, n_row)
    def _(d):
        right_copy(d).wait_send()


def solution(mesh):
    n_row, n_col = mesh.shape["row"], mesh.shape["col"]

    def local(pair, norm_in, shift_in, in_weight, norm_out, shift_out, out_weight):
        rows, cols, channels = pair.shape
        hidden = out_weight.shape[0]
        groups = n_row // n_col
        vmem = pl.BlockSpec(memory_space=pltpu.VMEM)
        return pl.pallas_call(
            functools.partial(kernel, n_row, n_col),
            out_shape=jax.ShapeDtypeStruct((rows, cols, channels), jnp.bfloat16),
            in_specs=[vmem] * 7,
            out_specs=vmem,
            scratch_shapes=[
                pltpu.VMEM((groups, rows, rows, hidden), jnp.bfloat16),
                pltpu.VMEM((n_row, rows, rows, hidden), jnp.bfloat16),
                pltpu.VMEM((n_row, rows, cols, hidden), jnp.bfloat16),
                pltpu.VMEM((rows, cols, channels), jnp.float32),
                pltpu.VMEM((rows, cols, hidden), jnp.float32),
                pltpu.SemaphoreType.DMA((groups * n_col,)),
                pltpu.SemaphoreType.DMA((n_row,)),
                pltpu.SemaphoreType.DMA((n_row,)),
                pltpu.SemaphoreType.DMA((n_row,)),
            ],
            compiler_params=pltpu.CompilerParams(collective_id=0, has_side_effects=True),
        )(
            pair, norm_in.reshape(1, -1), shift_in.reshape(1, -1), in_weight,
            norm_out.reshape(1, -1), shift_out.reshape(1, -1), out_weight,
        )

    in_specs = (P("row", "col", None), P(), P(), P(), P(), P(), P())
    return jax.shard_map(
        local, mesh=mesh, in_specs=in_specs, out_specs=P("row", "col", None), check_vma=False
    )
```

time: 72.2 us -> 21.4 us (0.30)
  blocking collectives: 50.7 us -> 0 us
  Pallas kernels: 0 us -> 19.8 us
  starting transfers between devices: 10.5 us -> 0 us
  waiting for transfers between devices: 3.76 us -> 0 us
  other arithmetic: 3.04 us -> 0 us
  matrix products: 1.67 us -> 0 us
    all_gather x2 -> x0, blocking collectives: 50.7 us -> none  [the longest x1 45.2 us: local(): right_full = lax.all_gather(right, 'row', axis=0, tiled=True)]
    pallas_call x0 -> x1, Pallas kernels: none -> 19.8 us  [local(): pl.pallas_call(functools.partial(kernel, n_row, n_col), out_shape=jax.Sha...]
    all_to_all x2 -> x0, starting transfers between devices: 10.5 us -> none  [the longest x1 6.25 us: local(): lax.all_to_all(sorted_parts, 'row', split_axis=1, concat_axis=0, tiled=True)]
    all_to_all x2 -> x0, waiting for transfers between devices: 3.76 us -> none  [the longest x1 3.76 us: local(): lax.all_to_all(sectioned, 'col', split_axis=1, concat_axis=1, tiled=True)]
    reduce_sum x4 -> x0, other arithmetic: 2.07 us -> none  [the longest x2 1.08 us: layer_norm(): spread = jnp.mean(jnp.square(values - center), axis=-1, keepdims=True)]
    dot_general x3 -> x0, matrix products: 1.67 us -> none  [the longest x1 0.84 us: local(): jnp.dot(mixed_normed.reshape(-1, hidden), out_weight, preferred_element_t...]
    unnamed x8 -> x1, local copies, waits for them, and re-layouts: 0.02 us -> 1.38 us
    convert_element_type x2 -> x0, other arithmetic: 0.94 us -> none  [the longest x1 0.88 us: local(): normed = layer_norm(pair, norm_in, shift_in).astype(jnp.bfloat16)]
  transfers between devices with their start and end apart: 2 -> 0, of which waited for: 1 -> 0; matrix products, arithmetic and copies ran while one was open for 0% -> 0% of each run, Pallas kernels for 0% -> 0%
where the time goes in v1:
time: 21.4 us; the launch traced here: 21.2 us
  Pallas kernels  19.8 us (93%)
  local copies, waits for them, and re-layouts  1.38 us (6%)
    pallas_call x1, Pallas kernels, local(): pl.pallas_call(functools.partial(kernel, n_row, n_col), out_shape=jax.Sha...  19.8 us
    unnamed x1, local copies, waits for them, and re-layouts  1.38 us

profile of v1, /device:TPU:0, one launch (start us, length us, event | category | flops | bytes accessed | tf_op | source)
XLA Modules:
  0.0 21.2 jit_solution(6622692516663992432)
XLA Ops:
  0.0 19.8 %shard_map.73 = bf16[8,16,128]{2,1,0:T(8,128)(2,1)} custom-call(bf16[8,16,128]{2,1,0:T(8,128)(2,1)} %pair_ref.1, f32[1,128]{1,0:T(1,128)} %bitcast.4, f32[1,128]{1,0:T(1,128)} %bitcast.5, bf16[128,640]{1,0:T(8,128)(2,1)} %w_in.1, f32[1,128]{1,0:T(1,128)} %bitcast.6, f32[1,128]{1,0:T(1,128)} %bitcast.7, bf16[128,128]{1,0:T(8,128)(2,1)} %w_out.1), custom_call_target="tpu_custom_call" | custom-call | tf_op jit(solution)/shard_map/pallas_call | solution.py:181
  19.8 1.4 %copy.9 = bf16[8,16,128]{2,1,0:T(8,128)(2,1)} copy(bf16[8,16,128]{2,1,0:T(8,128)(2,1)} %shard_map.73) | data formatting | bytes 65536

commit v2 on v1

--- a/solution.py
+++ b/solution.py
@@ -32,33 +32,63 @@
 
 
 def kernel(
-    n_row, n_col, pair_ref, gain_in, shift_in, w_in, gain_out, shift_out, w_out, out_ref,
-    left_own, left_all, right_all, gate_ref, mixed, left_send, left_recv, right_send, right_recv,
+    n_row, n_col, *refs
+):
+    sources, out_ref, held, fetch_sem = refs[:7], refs[7], refs[8:15], refs[15]
+    fetches = [
+        pltpu.make_async_copy(source, target, fetch_sem.at[i])
+        for i, (source, target) in enumerate(zip(sources, held))
+    ]
+    for fetch in fetches:
+        fetch.start()
+    body(n_row, n_col, fetches, *held, out_ref, *refs[16:])
+
+
+def body(
+    n_row, n_col, fetches, pair_ref, gain_in, shift_in, w_in, gain_out, shift_out, w_out, out_ref,
+    left_own, left_all, right_all, gate_ref, mixed,
+    left_send, left_pass, left_recv, right_send, right_pass, right_recv,
 ):
     rows, cols, channels = pair_ref.shape
     hidden = w_out.shape[0]
     groups = n_row // n_col
+    lines, chips = n_row // 2, n_col // 2
     r, c = lax.axis_index("row"), lax.axis_index("col")
     home = r // groups
-
+    u, x, core = r // 2, lax.rem(r, 2), lax.rem(c, 2)
+    pair_row = r + 1 - 2 * x
+    turn = jnp.where(2 * u < lines, 1, lines - 1)
+
+    def line(d):
+        return lax.rem(u + turn * d, lines)
+
+    first = c // 2 == home // 2
     barrier = pltpu.get_barrier_semaphore()
 
     def greet(row, col):
         pl.semaphore_signal(barrier, inc=1, device_id=(row, col), device_id_type=MESH)
 
-    @pl.loop(1, n_row)
-    def _(d):
-        greet(lax.rem(r + d, n_row), c)
-
-    @pl.loop(0, n_row)
-    def _(d):
-        row = lax.rem(r + d, n_row)
-
-        @pl.when(jnp.logical_or(row != r, home != c))
-        def _():
-            greet(row, home)
+    greet(pair_row, c)
+    for d in range(1, lines):
+        greet(2 * line(d) + x, c)
+
+    for p in range(2):
+        @pl.when(jnp.logical_or(c // 2 != home // 2, p != core))
+        def _():
+            greet(r, home // 2 * 2 + p)
+
+    @pl.when(first)
+    def _():
+        for d in range(lines):
+            source = 2 * line(d) + core
+
+            @pl.when(jnp.logical_or(source != r, home != c))
+            def _():
+                greet(source, home)
 
     step = fit(rows, max(1, 128 // cols))
+    for fetch in fetches:
+        fetch.wait()
 
     def project(t):
         at = pl.ds(t * step, step)
@@ -80,41 +110,76 @@
 
     loop(rows // step, project)
 
-    own = jnp.where(home == c, 1, 0)
-    pl.semaphore_wait(barrier, n_row - 1 + groups * n_col - own)
+    itself = jnp.logical_and(home == c, x == core)
+    expected = lines + groups - jnp.where(itself, 1, 0) + jnp.where(first, n_col - 1, 0)
+    pl.semaphore_wait(barrier, expected)
 
     def right_copy(d):
         return pltpu.make_async_remote_copy(
             src_ref=right_all.at[r], dst_ref=right_all.at[r],
             send_sem=right_send.at[d], recv_sem=right_recv.at[r],
-            device_id=(lax.rem(r + d, n_row), c), device_id_type=MESH,
-        )
-
-    def left_copy(g, d):
+            device_id=(2 * line(d) + x if d else pair_row, c), device_id_type=MESH,
+        )
+
+    def right_forward(d):
+        source = 2 * line(d) + x
+        return pltpu.make_async_remote_copy(
+            src_ref=right_all.at[source], dst_ref=right_all.at[source],
+            send_sem=right_pass.at[d], recv_sem=right_recv.at[source],
+            device_id=(pair_row, c), device_id_type=MESH,
+        )
+
+    def each_right(act):
+        for d in reversed(range(lines)):
+            act(right_copy(d))
+
+    def left_copy(g):
         return pltpu.make_async_remote_copy(
             src_ref=left_own.at[g], dst_ref=left_all.at[r],
-            send_sem=left_send.at[g * n_col + d], recv_sem=left_recv.at[r],
-            device_id=(c * groups + g, lax.rem(c + d, n_col)), device_id_type=MESH,
+            send_sem=left_send.at[g], recv_sem=left_recv.at[r],
+            device_id=(c * groups + g, c // 2 * 2 + x), device_id_type=MESH,
+        )
+
+    def left_forward(d, to):
+        source = 2 * line(d) + core
+        return pltpu.make_async_remote_copy(
+            src_ref=left_all.at[source], dst_ref=left_all.at[source],
+            send_sem=left_pass.at[d * n_col + to], recv_sem=left_recv.at[source],
+            device_id=(r, lax.rem(c + to, n_col)), device_id_type=MESH,
         )
 
     def each_left(act):
         for g in range(groups):
-            @pl.loop(0, n_col)
-            def _(d):
-                @pl.when(jnp.logical_or(d != 0, r != c * groups + g))
-                def _():
-                    act(left_copy(g, d))
-
+            @pl.when(jnp.logical_or(r != c * groups + g, x != core))
+            def _():
+                act(left_copy(g))
+
+    def arrive(buffer, semaphore, source):
+        pltpu.make_async_copy(buffer.at[source], buffer.at[source], semaphore.at[source]).wait()
+
+    each_right(lambda copy: copy.start())
     each_left(lambda copy: copy.start())
 
-    @pl.loop(1, n_row)
-    def _(d):
-        right_copy(d).start()
-
     for g in range(groups):
-        @pl.when(r == c * groups + g)
+        @pl.when(jnp.logical_and(r == c * groups + g, x == core))
         def _():
             left_all[r] = left_own[g]
+
+    for d in range(lines):
+        if d:
+            arrive(right_all, right_recv, 2 * line(d) + x)
+            right_forward(d).start()
+
+        @pl.when(first)
+        def _():
+            source = 2 * line(d) + core
+
+            @pl.when(jnp.logical_or(source != r, home != c))
+            def _():
+                arrive(left_all, left_recv, source)
+
+            for to in range(1, n_col):
+                left_forward(d, to).start()
 
     tile_k, tile_i, tile_j = fit(rows, 8), fit(rows, 8), fit(cols, 16)
     mixed[...] = jnp.zeros_like(mixed)
@@ -139,19 +204,18 @@
 
         loop(rows // tile_i, over_i)
 
-    @pl.loop(0, n_row)
-    def _(d):
-        s = lax.rem(r + n_row - d, n_row)
-
-        @pl.when(d != 0)
-        def _():
-            pltpu.make_async_copy(right_all.at[s], right_all.at[s], right_recv.at[s]).wait()
-
-        @pl.when(jnp.logical_or(d != 0, home != c))
-        def _():
-            pltpu.make_async_copy(left_all.at[s], left_all.at[s], left_recv.at[s]).wait()
-
-        accumulate(s)
+    for d in range(lines):
+        arrive(left_all, left_recv, 2 * line(d) + 1 - core)
+
+        @pl.when(jnp.logical_not(first))
+        def _():
+            arrive(left_all, left_recv, 2 * line(d) + core)
+
+        arrive(right_all, right_recv, 2 * line(d) + 1 - x)
+
+        @pl.loop(0, 2)
+        def _(e):
+            accumulate(2 * line(d) + e)
 
     def finish(t):
         at = pl.ds(t * step, step)
@@ -164,10 +228,15 @@
     loop(rows // step, finish)
 
     each_left(lambda copy: copy.wait_send())
-
-    @pl.loop(1, n_row)
-    def _(d):
-        right_copy(d).wait_send()
+    each_right(lambda copy: copy.wait_send())
+    for d in range(lines):
+        if d:
+            right_forward(d).wait_send()
+
+        @pl.when(first)
+        def _():
+            for to in range(1, n_col):
+                left_forward(d, to).wait_send()
 
 
 def solution(mesh):
@@ -181,17 +250,27 @@
         return pl.pallas_call(
             functools.partial(kernel, n_row, n_col),
             out_shape=jax.ShapeDtypeStruct((rows, cols, channels), jnp.bfloat16),
-            in_specs=[vmem] * 7,
+            in_specs=[pl.BlockSpec(memory_space=pl.ANY)] * 7,
             out_specs=vmem,
             scratch_shapes=[
+                pltpu.VMEM(pair.shape, pair.dtype),
+                pltpu.VMEM((1, channels), jnp.float32),
+                pltpu.VMEM((1, channels), jnp.float32),
+                pltpu.VMEM(in_weight.shape, in_weight.dtype),
+                pltpu.VMEM((1, hidden), jnp.float32),
+                pltpu.VMEM((1, hidden), jnp.float32),
+                pltpu.VMEM(out_weight.shape, out_weight.dtype),
+                pltpu.SemaphoreType.DMA((7,)),
                 pltpu.VMEM((groups, rows, rows, hidden), jnp.bfloat16),
                 pltpu.VMEM((n_row, rows, rows, hidden), jnp.bfloat16),
                 pltpu.VMEM((n_row, rows, cols, hidden), jnp.bfloat16),
                 pltpu.VMEM((rows, cols, channels), jnp.float32),
                 pltpu.VMEM((rows, cols, hidden), jnp.float32),
-                pltpu.SemaphoreType.DMA((groups * n_col,)),
+                pltpu.SemaphoreType.DMA((groups,)),
+                pltpu.SemaphoreType.DMA((n_row // 2 * n_col,)),
                 pltpu.SemaphoreType.DMA((n_row,)),
-                pltpu.SemaphoreType.DMA((n_row,)),
+                pltpu.SemaphoreType.DMA((n_row // 2,)),
+                pltpu.SemaphoreType.DMA((n_row // 2,)),
                 pltpu.SemaphoreType.DMA((n_row,)),
             ],
             compiler_params=pltpu.CompilerParams(collective_id=0, has_side_effects=True),

time: 21.4 us -> 17.1 us (0.80)
  Pallas kernels: 19.8 us -> 15.5 us
    pallas_call x1, Pallas kernels: 19.8 us -> 15.5 us  [local(): pl.pallas_call(functools.partial(kernel, n_row, n_col), out_shape=jax.Sha...]
where the time goes in v2:
time: 17.1 us; the launch traced here: 16.9 us
  Pallas kernels  15.5 us (91%)
  local copies, waits for them, and re-layouts  1.38 us (8%)
    pallas_call x1, Pallas kernels, local(): pl.pallas_call(functools.partial(kernel, n_row, n_col), out_shape=jax.Sha...  15.5 us
    unnamed x1, local copies, waits for them, and re-layouts  1.38 us

profile of v2, /device:TPU:0, one launch (start us, length us, event | category | flops | bytes accessed | tf_op | source)
XLA Modules:
  0.0 16.9 jit_solution(17126310089891643660)
XLA Ops:
  0.0 15.5 %shard_map.73 = bf16[8,16,128]{2,1,0:T(8,128)(2,1)} custom-call(bf16[8,16,128]{2,1,0:T(8,128)(2,1)} %refs_0_.1, f32[1,128]{1,0:T(1,128)} %bitcast.4, f32[1,128]{1,0:T(1,128)} %bitcast.5, bf16[128,640]{1,0:T(8,128)(2,1)} %refs_3_.1, f32[1,128]{1,0:T(1,128)} %bitcast.6, f32[1,128]{1,0:T(1,128)} %bitcast.7, bf16[128,128]{1,0:T(8,128)(2,1)} %refs_6_.1), custom_call_target="tpu_custom_call" | custom-call | tf_op jit(solution)/shard_map/pallas_call | solution.py:250
  15.5 1.4 %copy.9 = bf16[8,16,128]{2,1,0:T(8,128)(2,1)} copy(bf16[8,16,128]{2,1,0:T(8,128)(2,1)} %shard_map.73) | data formatting | bytes 65536

commit v3 on v2

--- a/solution.py
+++ b/solution.py
@@ -157,8 +157,8 @@
     def arrive(buffer, semaphore, source):
         pltpu.make_async_copy(buffer.at[source], buffer.at[source], semaphore.at[source]).wait()
 
+    each_left(lambda copy: copy.start())
     each_right(lambda copy: copy.start())
-    each_left(lambda copy: copy.start())
 
     for g in range(groups):
         @pl.when(jnp.logical_and(r == c * groups + g, x == core))
@@ -249,7 +249,7 @@
         vmem = pl.BlockSpec(memory_space=pltpu.VMEM)
         return pl.pallas_call(
             functools.partial(kernel, n_row, n_col),
-            out_shape=jax.ShapeDtypeStruct((rows, cols, channels), jnp.bfloat16),
+            out_shape=pltpu.VMEM((rows, cols, channels), jnp.bfloat16),
             in_specs=[pl.BlockSpec(memory_space=pl.ANY)] * 7,
             out_specs=vmem,
             scratch_shapes=[

time: 17.1 us -> 15.3 us (0.89)
  Pallas kernels: 15.5 us -> 14.6 us
  local copies, waits for them, and re-layouts: 1.38 us -> 0.62 us
    pallas_call x1, Pallas kernels: 15.5 us -> 14.6 us  [local(): pl.pallas_call(functools.partial(kernel, n_row, n_col), out_shape=pltpu.V...]
    unnamed x1, local copies, waits for them, and re-layouts: 1.38 us -> 0.62 us
where the time goes in v3:
time: 15.3 us; the launch traced here: 15.2 us
  Pallas kernels  14.6 us (95%)
  local copies, waits for them, and re-layouts  0.62 us (4%)
    pallas_call x1, Pallas kernels, local(): pl.pallas_call(functools.partial(kernel, n_row, n_col), out_shape=pltpu.V...  14.6 us
    unnamed x1, local copies, waits for them, and re-layouts  0.62 us

profile of v3, /device:TPU:0, one launch (start us, length us, event | category | flops | bytes accessed | tf_op | source)
XLA Modules:
  0.0 15.2 jit_solution(5610785927579434276)
XLA Ops:
  0.0 14.6 %shard_map.73 = bf16[8,16,128]{2,1,0:T(8,128)(2,1)S(1)} custom-call(bf16[8,16,128]{2,1,0:T(8,128)(2,1)} %refs_0_.1, f32[1,128]{1,0:T(1,128)} %bitcast.4, f32[1,128]{1,0:T(1,128)} %bitcast.5, bf16[128,640]{1,0:T(8,128)(2,1)} %refs_3_.1, f32[1,128]{1,0:T(1,128)} %bitcast.6, f32[1,128]{1,0:T(1,128)} %bitcast.7, bf16[128,128]{1,0:T(8,128)(2,1)} %refs_6_.1), custom_call_target="tpu_custom_call" | custom-call | tf_op jit(solution)/shard_map/pallas_call | solution.py:250
  14.6 0.6 %copy.9 = bf16[8,16,128]{2,1,0:T(8,128)(2,1)} copy(bf16[8,16,128]{2,1,0:T(8,128)(2,1)S(1)} %shard_map.73) | data formatting | bytes 65536

commit v4 on v3

--- a/solution.py
+++ b/solution.py
@@ -72,6 +72,11 @@
     for d in range(1, lines):
         greet(2 * line(d) + x, c)
 
+        @pl.when(jnp.abs(line(d) - u) > lines // 2)
+        def _():
+            greet(2 * line(d) + 1 - x, c)
+
+
     for p in range(2):
         @pl.when(jnp.logical_or(c // 2 != home // 2, p != core))
         def _():
@@ -112,6 +117,8 @@
 
     itself = jnp.logical_and(home == c, x == core)
     expected = lines + groups - jnp.where(itself, 1, 0) + jnp.where(first, n_col - 1, 0)
+    for d in range(1, lines):
+        expected += jnp.where(jnp.abs(line(d) - u) > lines // 2, 1, 0)
     pl.semaphore_wait(barrier, expected)
 
     def right_copy(d):
@@ -129,6 +136,22 @@
             device_id=(pair_row, c), device_id_type=MESH,
         )
 
+    def far(d):
+        return jnp.abs(line(d) - u) > lines // 2
+
+    def right_cross(d):
+        return pltpu.make_async_remote_copy(
+            src_ref=right_all.at[r], dst_ref=right_all.at[r],
+            send_sem=right_pass.at[d], recv_sem=right_recv.at[r],
+            device_id=(2 * line(d) + 1 - x, c), device_id_type=MESH,
+        )
+
+    def each_cross(act):
+        for d in range(1, lines):
+            @pl.when(far(d))
+            def _():
+                act(right_cross(d))
+
     def each_right(act):
         for d in reversed(range(lines)):
             act(right_copy(d))
@@ -157,8 +180,9 @@
     def arrive(buffer, semaphore, source):
         pltpu.make_async_copy(buffer.at[source], buffer.at[source], semaphore.at[source]).wait()
 
+    each_right(lambda copy: copy.start())
     each_left(lambda copy: copy.start())
-    each_right(lambda copy: copy.start())
+    each_cross(lambda copy: copy.start())
 
     for g in range(groups):
         @pl.when(jnp.logical_and(r == c * groups + g, x == core))
@@ -168,7 +192,11 @@
     for d in range(lines):
         if d:
             arrive(right_all, right_recv, 2 * line(d) + x)
-            right_forward(d).start()
+
+            @pl.when(jnp.logical_not(far(d)))
+            def _():
+                right_forward(d).start()
+
 
         @pl.when(first)
         def _():
@@ -229,9 +257,14 @@
 
     each_left(lambda copy: copy.wait_send())
     each_right(lambda copy: copy.wait_send())
+    each_cross(lambda copy: copy.wait_send())
     for d in range(lines):
         if d:
-            right_forward(d).wait_send()
+
+            @pl.when(jnp.logical_not(far(d)))
+            def _():
+                right_forward(d).wait_send()
+
 
         @pl.when(first)
         def _():

time: 15.3 us -> 14.9 us (0.974)
  the two profiles are of different devices: /device:TPU:0 before, /device:TPU:17 now
where the time goes in v4:
time: 14.9 us; the launch traced here: 14.7 us
  Pallas kernels  14.1 us (95%)
  local copies, waits for them, and re-layouts  0.62 us (4%)
    pallas_call x1, Pallas kernels, local(): pl.pallas_call(functools.partial(kernel, n_row, n_col), out_shape=pltpu.V...  14.1 us
    unnamed x1, local copies, waits for them, and re-layouts  0.62 us

profile of v4, /device:TPU:17, one launch (start us, length us, event | category | flops | bytes accessed | tf_op | source)
XLA Modules:
  0.0 14.7 jit_solution(13061406144208102737)
XLA Ops:
  0.0 14.1 %shard_map.73 = bf16[8,16,128]{2,1,0:T(8,128)(2,1)S(1)} custom-call(bf16[8,16,128]{2,1,0:T(8,128)(2,1)} %refs_0_.1, f32[1,128]{1,0:T(1,128)} %bitcast.4, f32[1,128]{1,0:T(1,128)} %bitcast.5, bf16[128,640]{1,0:T(8,128)(2,1)} %refs_3_.1, f32[1,128]{1,0:T(1,128)} %bitcast.6, f32[1,128]{1,0:T(1,128)} %bitcast.7, bf16[128,128]{1,0:T(8,128)(2,1)} %refs_6_.1), custom_call_target="tpu_custom_call" | custom-call | tf_op jit(solution)/shard_map/pallas_call | solution.py:283
  14.1 0.6 %copy.9 = bf16[8,16,128]{2,1,0:T(8,128)(2,1)} copy(bf16[8,16,128]{2,1,0:T(8,128)(2,1)S(1)} %shard_map.73) | data formatting | bytes 65536
